TPU v7x, 32 devices: a whole 2x2x4 slice. The times are simulated.
32 devices in a mesh: row: 4 (over z), col: 4 (over x, core), layer: 2 (over y).
Axes of the slice: x: 2, y: 2, z: 4, core: 2. Of those that a mesh axis runs over, the one named last changes fastest.
Arguments:
- left: bfloat16 [4096, 8192], P('row', ('col', 'layer')), may hold values from -6 to 6
- middle: bfloat16 [8192, 8192], P('row', 'col'), may hold values from -0.0625 to 0.0625
- right: bfloat16 [8192, 8192], P('row', 'col'), may hold values from -0.0625 to 0.0625
Outputs:
- product: bfloat16 [4096, 8192], P('row', ('col', 'layer'))
All inputs are finite; a program needn't handle non-finite values.
Results may differ from a plain program's by a relative error of at most 0.0049.
Values may be sent and summed in bfloat16 or wider, within the bound.
A program may use at most 128 MiB of HBM per device.

v0:
```python
import jax
import jax.numpy as jnp
from jax import lax
from jax.sharding import PartitionSpec as P


def multiply(left, right):
    width = left.shape[1]
    layers = lax.axis_size("layer")
    layer_index = lax.axis_index("layer")
    columns = right.shape[1]
    groups = right.shape[0] // width // layers
    shaped = right.reshape(groups, layers, width, columns)
    own_rows = lax.dynamic_index_in_dim(shaped, layer_index, 1, keepdims=False).reshape(
        groups * width, columns
    )
    right_all = lax.all_gather(own_rows, "row", axis=0, tiled=True)
    return jnp.dot(
        lax.all_gather(left, "col", axis=1, tiled=True),
        right_all,
        preferred_element_type=jnp.float32,
    )


def per_device(left, middle, right):
    partial_value = multiply(left, middle)
    total = lax.psum(partial_value, "layer")
    half = partial_value.shape[1] // lax.axis_size("layer")
    first = lax.dynamic_slice_in_dim(total, lax.axis_index("layer") * half, half, 1)
    first = first.astype(jnp.bfloat16)
    second = multiply(first, right)
    return lax.psum_scatter(second, "layer", scatter_dimension=1, tiled=True).astype(jnp.bfloat16)


def solution(mesh):
    return jax.shard_map(
        per_device,
        mesh=mesh,
        in_specs=(P("row", ("col", "layer")), P("row", "col"), P("row", "col")),
        out_specs=P("row", ("col", "layer")),
        check_vma=False,
    )
```

profile of v0, /device:TPU:0, one launch (start us, length us, event | category | flops | bytes accessed | tf_op | source)
XLA Modules:
  0.0 836.8 jit_solution(5286668010177135871)
XLA Ops:
  6.5 0.0 all-gather.7.cloned.1.call-start
  6.5 0.7 all-gather.7.cloned.1.call-update
  7.3 0.0 all-gather.11.cloned.1.call-start
  7.3 4.7 constant_dynamic-slice_fusion.1
  12.0 0.0 all-gather.11.cloned.1.call-update
  12.1 0.0 all-gather.13.cloned.1.call-start
  12.1 4.8 constant_dynamic-slice_fusion
  16.9 0.0 all-gather.13.cloned.1.call-update
  17.0 0.0 all-gather.9.cloned.1.call-start
  17.0 52.9 %all-gather.7.cloned.1.call-done = bf16[1024,4096]{1,0:T(8,128)(2,1)} async-done(((bf16[1024,1024]{1,0:T(8,128)(2,1)}), bf16[1024,4096]{1,0:T(8,128)(2,1)}) %all-gather.7.cloned.1.call-update) | async-done | bytes 8388624 | tf_op jit(solution)/shard_map/all_gather | solution.py:19
  69.9 288.4 %all-gather.11.cloned.1.call-done = bf16[1,1,4096,2048]{3,2,1,0:T(8,128)(2,1)} async-done(((bf16[1,1,1024,2048]{3,2,1,0:T(8,128)(2,1)}), bf16[1,1,4096,2048]{3,2,1,0:T(8,128)(2,1)}) %all-gather.11.cloned.1.call-update) | async-done | bytes 16777232 | tf_op jit(solution)/shard_map/all_gather | solution.py:17
  358.3 24.2 %fusion.4 = f32[1024,2048]{0,1:T(8,128)} fusion(bf16[1024,4096]{1,0:T(8,128)(2,1)} %all-gather.7.cloned.1.call-done, bf16[1,1,4096,2048]{3,2,1,0:T(8,128)(2,1)} %all-gather.11.cloned.1.call-done), kind=kOutput, calls=%fused_computation.4 | convolution fusion | flops 17179869184 | bytes 33554432 | tf_op jit(solution)/shard_map/dot_general | solution.py:18
  382.5 195.5 %all-reduce.1 = bf16[1024,2048]{0,1:T(8,128)(2,1)} all-reduce(f32[1024,2048]{0,1:T(8,128)} %fusion.4), channel_id=1, replica_groups=mesh['row'=4,'col'=4,'layer'=2] {'layer'}, use_global_device_ids=true, to_apply=%region_0.1 | all-reduce | flops 2097152 | bytes 12582912 | tf_op jit(solution)/shard_map/psum | solution.py:27
  578.0 3.1 dynamic-slice_convert_fusion
  581.1 0.0 all-gather.9.cloned.1.call-update
  581.1 0.0 reduce-scatter.2.cloned.1.call-start
  581.1 63.7 %all-gather.13.cloned.1.call-done = bf16[1,1,4096,2048]{3,2,1,0:T(8,128)(2,1)} async-done(((bf16[1,1,1024,2048]{3,2,1,0:T(8,128)(2,1)}), bf16[1,1,4096,2048]{3,2,1,0:T(8,128)(2,1)}) %all-gather.13.cloned.1.call-update) | async-done | bytes 16777232 | tf_op jit(solution)/shard_map/all_gather | solution.py:17
  644.8 57.9 %all-gather.9.cloned.1.call-done = bf16[1024,4096]{0,1:T(8,128)(2,1)} async-done(((bf16[1024,1024]{0,1:T(8,128)(2,1)}), bf16[1024,4096]{0,1:T(8,128)(2,1)}) %all-gather.9.cloned.1.call-update) | async-done | bytes 8388624 | tf_op jit(solution)/shard_map/all_gather | solution.py:19
  702.7 24.2 %fusion = f32[1024,2048]{1,0:T(8,128)} fusion(bf16[1024,4096]{0,1:T(8,128)(2,1)} %all-gather.9.cloned.1.call-done, bf16[1,1,4096,2048]{3,2,1,0:T(8,128)(2,1)} %all-gather.13.cloned.1.call-done), kind=kOutput, calls=%fused_computation | convolution fusion | flops 17179869184 | bytes 33554432 | tf_op jit(solution)/shard_map/dot_general | solution.py:18
  726.9 0.0 reduce-scatter.2.cloned.1.call-update
  726.9 99.5 %reduce-scatter.2.cloned.1.call-done = f32[1024,1024]{1,0:T(8,128)} async-done(((f32[1024,2048]{1,0:T(8,128)}), f32[1024,1024]{1,0:T(8,128)}) %reduce-scatter.2.cloned.1.call-update) | async-done | bytes 4194320 | tf_op jit(solution)/shard_map/reduce_scatter | solution.py:32
  826.4 3.8 convert_element_type.7
Async XLA Ops:
  6.5 63.4 %all-gather.7.cloned.1.call-start = ((), (), s32[]{:S(2)}) async-start(), calls=%async_computation.1 | async-start | bytes 10485760 | tf_op jit(solution)/shard_map/all_gather | solution.py:19
  7.3 351.0 %all-gather.11.cloned.1.call-start = ((), (), s32[]{:S(2)}) async-start(), calls=%async_computation.4 | async-start | bytes 20971520 | tf_op jit(solution)/shard_map/all_gather | solution.py:17
  12.1 632.8 %all-gather.13.cloned.1.call-start = ((), (), s32[]{:S(2)}) async-start(), calls=%async_computation.5 | async-start | bytes 20971520 | tf_op jit(solution)/shard_map/all_gather | solution.py:17
  17.0 685.7 %all-gather.9.cloned.1.call-start = ((), (), s32[]{:S(2)}) async-start(), calls=%async_computation.2 | async-start | bytes 10485760 | tf_op jit(solution)/shard_map/all_gather | solution.py:19
  581.1 245.3 %reduce-scatter.2.cloned.1.call-start = ((), (), s32[]{:S(2)}) async-start(), calls=%async_computation.3 | async-start | bytes 12582912 | tf_op jit(solution)/shard_map/reduce_scatter | solution.py:32
Sparse Core Ops, SparseCore 0:
  8.9 60.9 all-gather.6
  71.5 286.7 all-gather.10
  359.8 284.9 all-gather.12
  646.2 56.4 all-gather.8
  727.1 99.3 reduce-scatter.1
where the time goes:
time: 837 us
  waiting for transfers between devices  563 us (67%)
  blocking collectives  196 us (23%)
  matrix products  48.4 us (6%)
  between operations  13.1 us (2%)
  local copies, waits for them, and re-layouts  12.6 us (2%)
    all_gather x2, waiting for transfers between devices, multiply(): right_all = lax.all_gather(own_rows, 'row', axis=0, tiled=True)  352 us
    psum x1, blocking collectives, per_device(): total = lax.psum(partial_value, 'layer')  196 us
    all_gather x2, waiting for transfers between devices, multiply(): lax.all_gather(left, 'col', axis=1, tiled=True)  111 us
    reduce_scatter x1, waiting for transfers between devices, per_device(): lax.psum_scatter(second, 'layer', scatter_dimension=1, tiled=True)  99.5 us
    dot_general x2, matrix products, multiply(): jnp.dot(lax.all_gather(left, 'col', axis=1, tiled=True), right_all, prefe...  48.4 us
  transfers between devices with their start and end apart: 5, of which 5 were waited for; matrix products, arithmetic and copies ran while one was open for 4% of the time, Pallas kernels for 0%

commit v1 on v0

v1 whole, which is shorter than its diff:
```python
import functools

import jax
import jax.numpy as jnp
from jax import lax
from jax.experimental import pallas as pl
from jax.experimental.pallas import tpu as pltpu
from jax.sharding import PartitionSpec as P

CHUNKS = 4
TILE = 256
MESH = pl.DeviceIdType.MESH


def kernel(
    rows, cols, layers,
    left_ref, middle_ref, right_ref, out_ref,
    held, held2, rhs, sent, kept, near, far, near2,
    own_sem, home_sem, swap_sems, pair_sems, plane_sems, core_sems, near_sems, far_sems, near2_sems,
):
    group, side = rows // 2, cols // 2
    row, col, layer = lax.axis_index("row"), lax.axis_index("col"), lax.axis_index("layer")
    h, z = row // group, lax.rem(row, group)
    x, c = col // side, lax.rem(col, side)
    straight = h == x
    depth = middle_ref.shape[0]
    width = out_ref.shape[1]
    inner = left_ref.shape[1]
    chunk = left_ref.shape[0] // CHUNKS
    tile = min(TILE, width)

    def at(h_, x_):
        return (h_ * group + z, x_ * side + c, layer)

    def slot(col_, layer_):
        return col_ * layers + layer_

    sibling = col + 1 - 2 * lax.rem(col, 2)
    offsets = [(dc, dl) for dc in range(cols // 2) for dl in range(layers) if dc or dl]

    def moved(col_, dc, dl, sign):
        return lax.rem(col_ + sign * 2 * dc + cols, cols), lax.rem(layer + sign * dl + layers, layers)

    barrier = pltpu.get_barrier_semaphore()
    greeted = [at(1 - h, x), at(h, 1 - x), at(1 - h, 1 - x), (row, sibling, layer)]
    for shift in range(1, group):
        greeted.append((h * group + lax.rem(z + shift, group), col, layer))
    for dc, dl in offsets:
        greeted.append((row, *moved(col, dc, dl, 1)))
    for device in greeted:
        pl.semaphore_signal(barrier, inc=1, device_id=device, device_id_type=MESH)
    pl.semaphore_wait(barrier, len(greeted))

    me = slot(col, layer)

    def part(j):
        return pl.ds(j * chunk, chunk)

    def remote(src, dst, sems, device):
        return pltpu.make_async_remote_copy(
            src_ref=src, dst_ref=dst, send_sem=sems.at[0], recv_sem=sems.at[1],
            device_id=device, device_id_type=MESH,
        )

    home = pltpu.make_async_copy(left_ref, held.at[me], home_sem)

    def swap(j):
        return remote(
            left_ref.at[part(j)], held.at[slot(h * side + c, layer), part(j)],
            swap_sems.at[j], at(x, h),
        )

    columns = pl.ds(pl.multiple_of(layer * width, width), width)
    pieces = CHUNKS
    step = depth // pieces

    def own(which):
        ref = (middle_ref, right_ref)[which]
        return pltpu.make_async_copy(
            ref.at[:, columns], rhs.at[which, pl.ds(z * depth, depth)], own_sem.at[which]
        )

    def pair(which, piece, shift):
        ref = (middle_ref, right_ref)[which]
        return remote(
            ref.at[pl.ds(piece * step, step), columns],
            rhs.at[which, pl.ds(z * depth + piece * step, step)],
            pair_sems.at[which, piece, shift - 1],
            (h * group + lax.rem(z + shift, group), col, layer),
        )

    def pair_start(which, piece):
        for shift in range(1, group):
            pair(which, piece, shift).start()

    def pair_wait(which):
        for piece in range(pieces):
            for shift in range(1, group):
                pair(which, piece, shift).wait_recv()
        own(which).wait()

    buffers = (held, held2)

    def spread(phase, j, index):
        dc, dl = offsets[index]
        ref = buffers[phase].at[me, part(j)]
        return remote(ref, ref, plane_sems.at[phase, j, index], (row, *moved(col, dc, dl, 1)))

    def pass_on(phase, j, index):
        origin = me
        if index:
            dc, dl = offsets[index - 1]
            origin = slot(*moved(col, dc, dl, -1))
        ref = buffers[phase].at[origin, part(j)]
        return remote(ref, ref, core_sems.at[phase, j, index], (row, sibling, layer))

    def spread_start(phase, j):
        for index in range(len(offsets)):
            spread(phase, j, index).start()
        pass_on(phase, j, 0).start()

    def spread_finish(phase, j):
        for index in range(len(offsets)):
            spread(phase, j, index).wait_recv()
            pass_on(phase, j, index + 1).start()
        for index in range(len(offsets) + 1):
            pass_on(phase, j, index).wait_recv()

    def multiply(phase, j, piece, target):
        blocks = side * layers
        ref = buffers[phase]

        @pl.loop(0, width // tile)
        def _(n):
            across = pl.ds(pl.multiple_of(n * tile, tile), tile)
            total = jnp.zeros((chunk, tile), jnp.float32)
            for k in range(blocks):
                total += jnp.dot(
                    ref[piece * blocks + k, part(j), :],
                    rhs[phase, pl.ds(k * inner, inner), across],
                    preferred_element_type=jnp.float32,
                )
            target[part(j), across] = total.astype(target.dtype)

    def add(one, two, j, store):
        @pl.loop(0, chunk // 32)
        def _(i):
            span = pl.ds(pl.multiple_of(j * chunk + i * 32, 32), 32)
            value = one[span, :].astype(jnp.float32) + two[span, :].astype(jnp.float32)
            store(span, value.astype(jnp.bfloat16))

    def near_copy(j):
        target_row = jnp.where(straight, h, x)
        target_col = jnp.where(straight, 1 - x, x)
        return remote(sent.at[part(j)], near.at[part(j)], near_sems.at[j], at(target_row, target_col))

    def far_copy(j):
        return remote(kept.at[part(j)], far.at[part(j)], far_sems.at[j], at(x, 1 - x))

    def near2_copy(j):
        return remote(sent.at[part(j)], near2.at[part(j)], near2_sems.at[j], at(1 - h, x))

    @pl.when(straight)
    def _():
        home.start()

    @pl.when(jnp.logical_not(straight))
    def _():
        for j in range(CHUNKS):
            swap(j).start()

    own(0).start()
    own(1).start()
    for piece in range(pieces):
        pair_start(0, piece)

    @pl.when(straight)
    def _():
        home.wait()

    for j in range(CHUNKS):
        @pl.when(jnp.logical_not(straight))
        def _():
            swap(j).wait_recv()

        spread_start(0, j)

    def first_done(j):
        near_copy(j).wait_recv()

        def store(span, value):
            held2[me, span, :] = value

        @pl.when(straight)
        def _():
            add(near, kept, j, store)

        @pl.when(jnp.logical_not(straight))
        def _():
            far_copy(j).wait_recv()
            add(near, far, j, store)

        spread_start(1, j)

    for j in range(CHUNKS):
        spread_finish(0, j)
        if j == 0:
            pair_wait(0)
        multiply(0, j, 1 - h, sent)
        near_copy(j).start()
        multiply(0, j, h, kept)

        @pl.when(jnp.logical_not(straight))
        def _():
            far_copy(j).start()

        pair_start(1, j)
        if j:
            first_done(j - 1)
    first_done(CHUNKS - 1)

    def out_done(j):
        near2_copy(j).wait_recv()

        def store(span, value):
            out_ref[span, :] = value

        add(near2, kept, j, store)

    for j in range(CHUNKS):
        spread_finish(1, j)
        if j == 0:
            pair_wait(1)
        near_copy(j).wait_send()

        @pl.when(jnp.logical_not(straight))
        def _():
            far_copy(j).wait_send()

        multiply(1, j, 1 - h, sent)
        near2_copy(j).start()
        multiply(1, j, h, kept)
        if j:
            out_done(j - 1)
    out_done(CHUNKS - 1)

    @pl.when(jnp.logical_not(straight))
    def _():
        for j in range(CHUNKS):
            swap(j).wait_send()

    for j in range(CHUNKS):
        near2_copy(j).wait_send()
        for phase in range(2):
            for index in range(len(offsets)):
                spread(phase, j, index).wait_send()
            for index in range(len(offsets) + 1):
                pass_on(phase, j, index).wait_send()
    for which in range(2):
        for piece in range(pieces):
            for shift in range(1, group):
                pair(which, piece, shift).wait_send()


def per_device(left, middle, right):
    rows, cols, layers = (lax.axis_size(name) for name in ("row", "col", "layer"))
    height, inner = left.shape
    width = right.shape[1] // layers
    depth = right.shape[0]
    group = rows // 2
    partners = cols // 2 * layers - 1
    bf16 = jnp.bfloat16
    anywhere = pl.BlockSpec(memory_space=pl.ANY)
    dma = pltpu.SemaphoreType.DMA
    return pl.pallas_call(
        functools.partial(kernel, rows, cols, layers),
        out_shape=jax.ShapeDtypeStruct((height, width), bf16),
        in_specs=[anywhere] * 3,
        out_specs=pl.BlockSpec(memory_space=pltpu.VMEM),
        scratch_shapes=[
            pltpu.VMEM((cols * layers, height, inner), bf16),
            pltpu.VMEM((cols * layers, height, inner), bf16),
            pltpu.VMEM((2, group * depth, width), bf16),
        ]
        + [pltpu.VMEM((height, width), bf16)] * 5
        + [
            dma((2,)),
            dma,
            dma((CHUNKS, 2)),
            dma((2, CHUNKS, max(group - 1, 1), 2)),
            dma((2, CHUNKS, partners, 2)),
            dma((2, CHUNKS, partners + 1, 2)),
            dma((CHUNKS, 2)),
            dma((CHUNKS, 2)),
            dma((CHUNKS, 2)),
        ],
        compiler_params=pltpu.CompilerParams(
            collective_id=0, has_side_effects=True, vmem_limit_bytes=67043328
        ),
    )(left, middle, right)


def solution(mesh):
    return jax.shard_map(
        per_device,
        mesh=mesh,
        in_specs=(P("row", ("col", "layer")), P("row", "col"), P("row", "col")),
        out_specs=P("row", ("col", "layer")),
        check_vma=False,
    )
```

time: 837 us -> 423 us (0.51)
  waiting for transfers between devices: 563 us -> 0 us
  Pallas kernels: 0 us -> 420 us
  blocking collectives: 196 us -> 0 us
  matrix products: 48.4 us -> 0 us
  between operations: 13.1 us -> 0.01 us
  local copies, waits for them, and re-layouts: 12.6 us -> 3.08 us
    all_gather x4 -> x0, waiting for transfers between devices: 463 us -> none  [the longest x2 352 us: multiply(): right_all = lax.all_gather(own_rows, 'row', axis=0, tiled=True)]
    pallas_call x0 -> x1, Pallas kernels: none -> 420 us  [per_device(): pl.pallas_call(functools.partial(kernel, rows, cols, layers), out_shape=j...]
    psum x1 -> x0, blocking collectives: 196 us -> none  [per_device(): total = lax.psum(partial_value, 'layer')]
    reduce_scatter x1 -> x0, waiting for transfers between devices: 99.5 us -> none  [per_device(): lax.psum_scatter(second, 'layer', scatter_dimension=1, tiled=True)]
    dot_general x2 -> x0, matrix products: 48.4 us -> none  [multiply(): jnp.dot(lax.all_gather(left, 'col', axis=1, tiled=True), right_all, prefe...]
    dynamic_slice x2 -> x0, local copies, waits for them, and re-layouts: 9.56 us -> none  [multiply(): lax.dynamic_index_in_dim(shaped, layer_index, 1, keepdims=False)]
  transfers between devices with their start and end apart: 5 -> 0, of which waited for: 5 -> 0; matrix products, arithmetic and copies ran while one was open for 4% -> 0% of each run, Pallas kernels for 0% -> 0%
where the time goes in v1:
time: 423 us
  Pallas kernels  420 us (99%)
    pallas_call x1, Pallas kernels, per_device(): pl.pallas_call(functools.partial(kernel, rows, cols, layers), out_shape=j...  420 us

profile of v1, /device:TPU:0, one launch (start us, length us, event | category | flops | bytes accessed | tf_op | source)
XLA Modules:
  0.0 422.7 jit_solution(4300253242156584199)
XLA Ops:
  0.0 419.6 %shard_map.37 = bf16[1024,1024]{1,0:T(8,128)(2,1)} custom-call(bf16[1024,1024]{1,0:T(8,128)(2,1)} %left_ref.1, bf16[2048,2048]{1,0:T(8,128)(2,1)} %middle_ref.1, bf16[2048,2048]{1,0:T(8,128)(2,1)} %right_ref.1), custom_call_target="tpu_custom_call" | custom-call | tf_op jit(solution)/shard_map/pallas_call | solution.py:275
  419.6 3.1 copy.5
